TPU v7x, 32 devices: a whole 2x2x4 slice. The times are simulated.
32 devices in a mesh: row: 16 (over z, y, x), col: 2 (over core).
Axes of the slice: x: 2, y: 2, z: 4, core: 2. Of those that a mesh axis runs over, the one named last changes fastest.
Arguments:
- lanczos_now: float32 [1, 256, 1024], P(None, 'row', 'col'), may hold values from -80 to 80, as said below
- lanczos_prev: float32 [1, 256, 1024], P(None, 'row', 'col'), may hold values from -6 to 6
- beta_prev: float32 [1], replicated, may hold values from 0.3 to 1.5
- valence_energy: float32 [256], P('row'), may hold values from -1.5 to -0.5
- conduction_energy: float32 [1024], P('col'), may hold values from 0.5 to 2.5
- valence_panel: float32 [16384, 256], P(('row', 'col')), may hold values from -0.375 to 0.375
- conduction_panel: float32 [16384, 1024], P(('row', 'col')), may hold values from -0.1875 to 0.1875
- screened_coulomb: float32 [16384, 16384], P('row', 'col'), may hold values from -0.046875 to 0.046875
- bare_coulomb: float32 [16384, 16384], P('row', 'col'), may hold values from -0.046875 to 0.046875
Outputs:
- lanczos_next: float32 [1, 256, 1024], P(None, 'row', 'col')
- coefficients: float32 [1, 2], replicated
Inputs may be any that keep to these rules, and one draw needn't show every extreme that they name: `lanczos_now`: real entries; the vectors of a chain are not normalized.
All inputs are finite; a program needn't handle non-finite values.
Results may differ from a plain program's by a relative error of at most 0.0002.
Values sent between devices are 32-bit elements; how exact they have to be, the bound alone decides.
A program may use at most 192 MiB of HBM per device.

v0:
```python
import jax
import jax.numpy as jnp
from jax import lax
from jax.sharding import PartitionSpec as P

V = 256
C = 1024
precise = lax.Precision.HIGHEST
epsilon = 1e-06


def per_device(
    lanczos_now,
    lanczos_prev,
    beta_prev,
    valence_energy,
    conduction_energy,
    valence_panel,
    conduction_panel,
    screened_coulomb,
    bare_coulomb,
):
    column_points = screened_coulomb.shape[1]
    wider = lax.all_gather(lanczos_now, "col", axis=2, tiled=True)
    vectors = lax.all_gather(wider, "row", axis=1, tiled=True)
    products = jnp.einsum("pv,kvc->pkc", valence_panel, vectors, precision=precise)
    density = jnp.sum(products * conduction_panel[:, None, :], axis=2)
    pair_local = jnp.einsum("pc,kvc->pkv", conduction_panel, vectors, precision=precise)
    every_panel, every_density = (
        lax.all_gather(valence_panel, ("row", "col"), axis=0, tiled=True),
        lax.all_gather(density, ("row", "col"), axis=0, tiled=True),
    )
    first_point = lax.axis_index("col") * column_points
    panel = lax.dynamic_slice_in_dim(every_panel, first_point, column_points, 0)
    far_density = lax.dynamic_slice_in_dim(every_density, first_point, column_points, 0)
    pair_terms = (
        jnp.einsum(
            "mkv,nv->mkn",
            lax.all_gather(pair_local, "col", axis=0, tiled=True),
            panel,
            precision=precise,
        )
        * screened_coulomb[:, None, :]
    )
    screened = jnp.einsum("mkn,nv->mkv", pair_terms, panel, precision=precise)
    potential = jnp.dot(bare_coulomb, far_density, precision=precise)
    direct_rows, local_potential = (
        lax.psum_scatter(screened, "col", scatter_dimension=0, tiled=True),
        lax.psum_scatter(potential, "col", scatter_dimension=0, tiled=True),
    )
    weighted = local_potential[:, :, None] * conduction_panel[:, None, :]
    bare_term = jnp.einsum("pv,pkc->vkc", valence_panel, weighted, precision=precise)
    screened_term = jnp.einsum("mkv,mc->vkc", direct_rows, conduction_panel, precision=precise)
    band_rows = lax.psum_scatter(
        2.0 * bare_term - screened_term, "row", scatter_dimension=0, tiled=True
    )
    kernel_part = lax.psum_scatter(band_rows, "col", scatter_dimension=2, tiled=True)
    kernel_part = jnp.transpose(kernel_part, (1, 0, 2))
    gaps = conduction_energy[None, None, :] - valence_energy[None, :, None]
    image = gaps * lanczos_now + kernel_part
    inverse_size = 1.0 / (V * C)
    sum_qu, sum_qq = lax.psum(
        (
            jnp.sum(lanczos_now * image, axis=(1, 2)),
            jnp.sum(lanczos_now * lanczos_now, axis=(1, 2)),
        ),
        ("row", "col"),
    )
    coef_alpha = sum_qu * inverse_size / (sum_qq * inverse_size + epsilon)
    resid = (
        image - coef_alpha[:, None, None] * lanczos_now - beta_prev[:, None, None] * lanczos_prev
    )
    sum_ww = lax.psum(jnp.sum(resid * resid, axis=(1, 2)), ("row", "col"))
    mean_ww = sum_ww * inverse_size
    beta_next = jnp.sqrt(mean_ww + epsilon)
    return (resid / beta_next[:, None, None], jnp.stack([coef_alpha, beta_next], axis=1))


def solution(mesh):
    placed = (
        P(None, "row", "col"),
        P(None, "row", "col"),
        P(),
        P("row"),
        P("col"),
        P(("row", "col"), None),
        P(("row", "col"), None),
        P("row", "col"),
        P("row", "col"),
    )
    return jax.shard_map(
        per_device,
        mesh=mesh,
        in_specs=placed,
        out_specs=(P(None, "row", "col"), P()),
        check_vma=False,
    )
```

profile of v0, /device:TPU:0, one launch (start us, length us, event | category | flops | bytes accessed | tf_op | source)
XLA Modules:
  0.0 517.7 jit_solution(11263954735266079760)
XLA Ops:
  7.2 3.5 all_gather.15
  10.8 57.7 %all-gather.7.cloned.1.call-done = f32[1,256,1024]{2,1,0:T(8,128)} async-done(((f32[1,16,1024]{2,1,0:T(8,128)}), f32[1,256,1024]{2,1,0:T(8,128)}) %all-gather.7.cloned.1.call-update) | async-done | bytes 1048592 | tf_op jit(solution)/shard_map/all_gather | solution.py:25
  68.6 4.5 fusion.21
  73.2 0.7 all-gather.9.cloned.1.call-update
  73.9 4.1 multiply_reduce_fusion
  78.0 39.9 %all-gather.2 = f32[32,1,512]{2,1,0:T(1,128)S(1)} all-gather(f32[1,1,512]{2,1,0:T(1,128)S(1)} %bitcast.62), channel_id=2, replica_groups=mesh['row'=16,'col'=2] {'row','col'}, dimensions={0}, use_global_device_ids=true | all-gather | bytes 67584 | tf_op jit(solution)/shard_map/all_gather | solution.py:31
  117.9 30.6 %convolution_bitcast_fusion.1 = f32[1024,1]{1,0:T(8,128)} fusion(f32[8192,1]{0,1:T(1,128)S(1)} %bitcast.57, f32[1024,8192]{1,0:T(8,128)} %param.17), kind=kOutput, calls=%fused_computation.15 | convolution fusion | flops 100663296 | bytes 33591296 | tf_op jit(solution)/shard_map/dot_general | solution.py:46
  148.5 0.2 reduce-scatter.8.cloned.1.call-start
  148.7 51.1 %all-gather.9.cloned.1.call-done = f32[16384,256]{1,0:T(8,128)} async-done(((f32[512,256]{1,0:T(8,128)}), f32[16384,256]{1,0:T(8,128)}) %all-gather.9.cloned.1.call-update) | async-done | bytes 16777232 | tf_op jit(solution)/shard_map/all_gather | solution.py:30
  199.8 32.1 %fusion.3 = f32[1024,8192]{1,0:T(8,128)} fusion(f32[1024,256]{1,0:T(8,128)} %all-gather.11.cloned.1.call-done, f32[16384,256]{1,0:T(8,128)} %all-gather.9.cloned.1.call-done, s32[]{:T(128)S(6)} %select_n.4), kind=kOutput, calls=%fused_computation.4 | convolution fusion | flops 25769803776 | bytes 42991620 | tf_op jit(solution)/shard_map/mkv,nv->mkn/dot_general | solution.py:37
  231.9 33.1 %fusion.13 = f32[1024,1,256]{2,0,1:T(8,128)} fusion(f32[16384,256]{1,0:T(8,128)} %all-gather.9.cloned.1.call-done, s32[]{:T(128)S(6)} %select_n.4, f32[1024,8192]{1,0:T(8,128)} %fusion.3, f32[1024,8192]{1,0:T(8,128)} %param.16), kind=kOutput, calls=%fused_computation.13 | convolution fusion | flops 25778192384 | bytes 76546048 | tf_op jit(solution)/shard_map/mkn,nv->mkv/dot_general | solution.py:45
  265.0 0.3 all-reduce.4.cloned.1.call-start
  265.3 1.1 copy.43
  266.4 5.4 %reduce-scatter.8.cloned.1.call-done = f32[512,1,256]{2,0,1:T(8,128)} async-done(((f32[1024,1,256]{2,0,1:T(8,128)}), f32[512,1,256]{2,0,1:T(8,128)}) %reduce-scatter.8.cloned.1.call-update) | async-done | bytes 524304 | tf_op jit(solution)/shard_map/reduce_scatter | solution.py:48
  271.8 4.5 convolution_bitcast_fusion
  276.3 4.6 fusion.18
  280.9 3.6 copy.36
  284.6 0.6 dynamic-slice.1
  285.8 112.5 %all-reduce.4.cloned.1.call-done = f32[256,1,1024]{2,1,0:T(1,128)} async-done(((f32[256,1,1024]{2,1,0:T(1,128)}), f32[256,1,1024]{2,1,0:T(1,128)}) %all-reduce.4.cloned.1.call-update) | async-done | bytes 1048592
  398.3 0.8 constant_dynamic-slice_fusion
  399.2 5.9 %copy.44 = f32[16,1,1024]{1,0,2:T(8,128)} copy(f32[16,1,1024]{2,1,0:T(1,128)S(1)} %constant_dynamic-slice_fusion) | data formatting | bytes 131072
  405.0 6.5 %bitcast_reduce_fusion = f32[1024,16]{1,0:T(8,128)} fusion(f32[16,1,1024]{1,0,2:T(8,128)} %copy.44), kind=kLoop, calls=%fused_computation.2 | loop fusion | bytes 131072
  412.2 0.6 multiply_reduce_fusion.2
  412.8 5.9 %reduce-scatter.12.cloned.1.call-done = f32[512,16]{1,0:T(8,128)} async-done(((f32[1024,16]{1,0:T(8,128)}), f32[512,16]{1,0:T(8,128)}) %reduce-scatter.12.cloned.1.call-update) | async-done | bytes 32784
  418.7 3.4 reshape_bitcast_fusion
  422.1 2.8 copy.45
  425.0 0.8 multiply_reduce_fusion.3
  425.8 40.6 %all-reduce.1 = (f32[1]{0:T(128)}, f32[1]{0:T(128)}) all-reduce(f32[1]{0:T(128)} %bitcast.15, f32[1]{0:T(128)} %bitcast.16), channel_id=1, replica_groups=mesh['row'=16,'col'=2] {'row','col'}, use_global_device_ids=true, to_apply=%region_6.0 | all-reduce | flops 2 | bytes 16 | tf_op jit(solution)/shard_map/psum | solution.py:62
  467.8 0.7 multiply_reduce_fusion.1
  468.5 40.5 %psum.23 = f32[1]{0:T(128)} all-reduce(f32[1]{0:T(128)} %bitcast.19), channel_id=1, replica_groups=mesh['row'=16,'col'=2] {'row','col'}, use_global_device_ids=true, to_apply=%region_10.0 | all-reduce | flops 1 | bytes 8 | tf_op jit(solution)/shard_map/psum | solution.py:73
  509.6 0.6 copy.40
  510.2 0.6 pad_maximum_fusion
  (29 shorter events, 0.4 us)
Async XLA Ops:
  7.2 61.4 %all-gather.7.cloned.1.call-start = ((), (), s32[]{:S(2)}) async-start(), calls=%async_computation.3 | async-start | bytes 1114112 | tf_op jit(solution)/shard_map/all_gather | solution.py:25
  10.8 137.9 %all-gather.11.cloned.1.call-start = ((), (), s32[]{:S(2)}) async-start(), calls=%async_computation.6 | async-start | bytes 1572864 | tf_op jit(solution)/shard_map/all_gather | solution.py:39
  73.1 126.7 %all-gather.9.cloned.1.call-start = ((), (), s32[]{:S(2)}) async-start(), calls=%async_computation.4 | async-start | bytes 17301504 | tf_op jit(solution)/shard_map/all_gather | solution.py:30
  73.8 191.5 %reduce-scatter.10.cloned.1.call-start = ((), (), s32[]{:S(2)}) async-start(), calls=%async_computation.7 | async-start | bytes 786432
  148.5 123.3 %reduce-scatter.8.cloned.1.call-start = ((), (), s32[]{:S(2)}) async-start(), calls=%async_computation.5 | async-start | bytes 1572864 | tf_op jit(solution)/shard_map/reduce_scatter | solution.py:48
  231.9 39.9 %copy-start = (f32[512,1024]{1,0:T(8,128)S(1)}, f32[512,1024]{1,0:T(8,128)}, u32[]{:S(2)}) copy-start(f32[512,1024]{1,0:T(8,128)} %param.15) | copy-start | bytes 6291460
  231.9 44.4 %copy-start.1 = (f32[512,256]{1,0:T(8,128)S(1)}, f32[512,256]{1,0:T(8,128)}, u32[]{:S(2)}) copy-start(f32[512,256]{1,0:T(8,128)} %param.14) | copy-start | bytes 1572868
  265.0 19.6 %copy-start.6 = (u32[32]{0:T(128)S(1)}, u32[32]{0:T(128)}, u32[]{:S(2)}) copy-start(u32[32]{0:T(128)} %constant.20) | copy-start | bytes 388
  265.0 133.3 %all-reduce.4.cloned.1.call-start = ((), (), s32[]{:S(2)}) async-start(), calls=%async_computation.9 | async-start | bytes 2097152
  284.5 134.2 %reduce-scatter.12.cloned.1.call-start = ((), (), s32[]{:S(2)}) async-start(), calls=%async_computation.8 | async-start | bytes 786432
  399.2 13.0 %copy-start.2 = (f32[1,16,512]{2,1,0:T(8,128)S(1)}, f32[1,16,512]{2,1,0:T(8,128)}, u32[]{:S(2)}) copy-start(f32[1,16,512]{2,1,0:T(8,128)} %param.9) | copy-start | bytes 98308
  405.0 20.0 %copy-start.4 = (f32[512]{0:T(512)S(1)}, f32[512]{0:T(512)}, u32[]{:S(2)}) copy-start(f32[512]{0:T(512)} %param.13) | copy-start | bytes 6148
  405.0 20.0 %copy-start.5 = (f32[16]{0:T(128)S(1)}, f32[16]{0:T(128)}, u32[]{:S(2)}) copy-start(f32[16]{0:T(128)} %param.12) | copy-start | bytes 196
  405.0 62.8 %copy-start.3 = (f32[1,16,512]{2,1,0:T(8,128)S(1)}, f32[1,16,512]{2,1,0:T(8,128)}, u32[]{:S(2)}) copy-start(f32[1,16,512]{2,1,0:T(8,128)} %param.10) | copy-start | bytes 98308
Sparse Core Ops, SparseCore 0:
  10.9 57.6 all-gather.6
  73.2 7.8 all-gather.10
  84.0 115.7 all-gather.8
  201.9 6.1 reduce-scatter.9
  265.1 6.5 reduce-scatter.7
  284.6 113.6 all-reduce.3
  411.7 6.9 reduce-scatter.11
where the time goes:
time: 518 us
  waiting for transfers between devices  233 us (45%)
  blocking collectives  125 us (24%)
  matrix products  113 us (22%)
  local copies, waits for them, and re-layouts  25.4 us (5%)
  between operations  17.6 us (3%)
    unnamed x10, waiting for transfers between devices  119 us
    all_gather x1, waiting for transfers between devices, per_device(): vectors = lax.all_gather(wider, 'row', axis=1, tiled=True)  57.7 us
    all_gather x1, waiting for transfers between devices, per_device(): lax.all_gather(valence_panel, ('row', 'col'), axis=0, tiled=True)  51.1 us
    psum x1, blocking collectives, per_device(): lax.psum((jnp.sum(lanczos_now * image, axis=(1, 2)), jnp.sum(lanczos_now...  40.6 us
    psum x1, blocking collectives, per_device(): sum_ww = lax.psum(jnp.sum(resid * resid, axis=(1, 2)), ('row', 'col'))  40.5 us
    all_gather x1, blocking collectives, per_device(): lax.all_gather(density, ('row', 'col'), axis=0, tiled=True)  39.9 us
    dot_general x1, matrix products, per_device(): screened = jnp.einsum('mkn,nv->mkv', pair_terms, panel, precision=precise)  33.1 us
    dot_general x1, matrix products, per_device(): jnp.einsum('mkv,nv->mkn', lax.all_gather(pair_local, 'col', axis=0, tiled...  32.1 us
  transfers between devices with their start and end apart: 7, of which 5 were waited for; matrix products, arithmetic and copies ran while one was open for 20% of the time, Pallas kernels for 0%

commit v1 on v0

--- a/solution.py
+++ b/solution.py
@@ -22,7 +22,12 @@
 ):
     column_points = screened_coulomb.shape[1]
     wider = lax.all_gather(lanczos_now, "col", axis=2, tiled=True)
-    vectors = lax.all_gather(wider, "row", axis=1, tiled=True)
+    ring = [wider]
+    for hop in range(15):
+        ring.append(lax.ppermute(ring[-1], "row", [(dev, (dev + 1) % 16) for dev in range(16)]))
+    vectors = jnp.roll(
+        jnp.concatenate(ring[::-1], axis=1), (lax.axis_index("row") + 1) * ring[0].shape[1], axis=1
+    )
     products = jnp.einsum("pv,kvc->pkc", valence_panel, vectors, precision=precise)
     density = jnp.sum(products * conduction_panel[:, None, :], axis=2)
     pair_local = jnp.einsum("pc,kvc->pkv", conduction_panel, vectors, precision=precise)

time: 518 us -> 609 us (1.18); the launches traced: 518 us -> 602 us
  waiting for transfers between devices: 233 us -> 289 us
  matrix products: 113 us -> 139 us
    ppermute x0 -> x15, waiting for transfers between devices: none -> 117 us  [per_device(): lax.ppermute(ring[-1], 'row', [(dev, (dev + 1) % 16) for dev in range(16)])]
    all_gather x1 -> x0, waiting for transfers between devices: 57.7 us -> none  [per_device(): vectors = lax.all_gather(wider, 'row', axis=1, tiled=True)]
    dot_general x1, matrix products: 32.1 us -> 58.3 us  [per_device(): jnp.einsum('mkv,nv->mkn', lax.all_gather(pair_local, 'col', axis=0, tiled...]
    unnamed x22 -> x56, local copies, waits for them, and re-layouts: 21.8 us -> 25.4 us
    unnamed x10 -> x9, waiting for transfers between devices: 119 us -> 119 us
  transfers between devices with their start and end apart: 7 -> 21, of which waited for: 5 -> 19; matrix products, arithmetic and copies ran while one was open for 20% -> 22% of each run, Pallas kernels for 0% -> 0%
where the time goes in v1:
time: 609 us; the launch traced here: 602 us
  waiting for transfers between devices  289 us (47%)
  matrix products  139 us (23%)
  blocking collectives  121 us (20%)
  local copies, waits for them, and re-layouts  29 us (5%)
  between operations  18.2 us (3%)
    unnamed x9, waiting for transfers between devices  119 us
    ppermute x15, waiting for transfers between devices, per_device(): lax.ppermute(ring[-1], 'row', [(dev, (dev + 1) % 16) for dev in range(16)])  117 us
    dot_general x1, matrix products, per_device(): jnp.einsum('mkv,nv->mkn', lax.all_gather(pair_local, 'col', axis=0, tiled...  58.3 us
    all_gather x1, waiting for transfers between devices, per_device(): lax.all_gather(valence_panel, ('row', 'col'), axis=0, tiled=True)  47.2 us
    psum x1, blocking collectives, per_device(): lax.psum((jnp.sum(lanczos_now * image, axis=(1, 2)), jnp.sum(lanczos_now...  40.6 us
    psum x1, blocking collectives, per_device(): sum_ww = lax.psum(jnp.sum(resid * resid, axis=(1, 2)), ('row', 'col'))  40.4 us
    all_gather x1, blocking collectives, per_device(): lax.all_gather(density, ('row', 'col'), axis=0, tiled=True)  37.6 us
    dot_general x1, matrix products, per_device(): screened = jnp.einsum('mkn,nv->mkv', pair_terms, panel, precision=precise)  32.9 us
  transfers between devices with their start and end apart: 21, of which 19 were waited for; matrix products, arithmetic and copies ran while one was open for 22% of the time, Pallas kernels for 0%

profile of v1, /device:TPU:0, one launch (start us, length us, event | category | flops | bytes accessed | tf_op | source)
XLA Modules:
  0.0 602.1 jit_solution(9812892258527024276)
XLA Ops:
  12.3 6.4 %collective-permute-done = f32[1,16,1024]{2,1,0:T(8,128)S(1)} collective-permute-done((f32[1,16,1024]{2,1,0:T(8,128)S(1)}, f32[1,16,1024]{2,1,0:T(8,128)S(1)}, u32[]{:S(2)}, u32[]{:S(2)}) %collective-permute-start) | collective-permute-done | bytes 65568 | tf_op jit(solution)/shard_map/ppermute | solution.py:27
  18.7 7.9 %collective-permute-done.1 = f32[1,16,1024]{2,1,0:T(8,128)S(1)} collective-permute-done((f32[1,16,1024]{2,1,0:T(8,128)S(1)}, f32[1,16,1024]{2,1,0:T(8,128)S(1)}, u32[]{:S(2)}, u32[]{:S(2)}) %collective-permute-start.1) | collective-permute-done | bytes 65568 | tf_op jit(solution)/shard_map/ppermute | solution.py:27
  26.5 7.9 %collective-permute-done.2 = f32[1,16,1024]{2,1,0:T(8,128)S(1)} collective-permute-done((f32[1,16,1024]{2,1,0:T(8,128)S(1)}, f32[1,16,1024]{2,1,0:T(8,128)S(1)}, u32[]{:S(2)}, u32[]{:S(2)}) %collective-permute-start.2) | collective-permute-done | bytes 65568 | tf_op jit(solution)/shard_map/ppermute | solution.py:27
  34.4 7.9 %collective-permute-done.3 = f32[1,16,1024]{2,1,0:T(8,128)S(1)} collective-permute-done((f32[1,16,1024]{2,1,0:T(8,128)S(1)}, f32[1,16,1024]{2,1,0:T(8,128)S(1)}, u32[]{:S(2)}, u32[]{:S(2)}) %collective-permute-start.3) | collective-permute-done | bytes 65568 | tf_op jit(solution)/shard_map/ppermute | solution.py:27
  42.2 7.9 %collective-permute-done.4 = f32[1,16,1024]{2,1,0:T(8,128)S(1)} collective-permute-done((f32[1,16,1024]{2,1,0:T(8,128)S(1)}, f32[1,16,1024]{2,1,0:T(8,128)S(1)}, u32[]{:S(2)}, u32[]{:S(2)}) %collective-permute-start.4) | collective-permute-done | bytes 65568 | tf_op jit(solution)/shard_map/ppermute | solution.py:27
  50.1 7.9 %collective-permute-done.5 = f32[1,16,1024]{2,1,0:T(8,128)S(1)} collective-permute-done((f32[1,16,1024]{2,1,0:T(8,128)S(1)}, f32[1,16,1024]{2,1,0:T(8,128)S(1)}, u32[]{:S(2)}, u32[]{:S(2)}) %collective-permute-start.5) | collective-permute-done | bytes 65568 | tf_op jit(solution)/shard_map/ppermute | solution.py:27
  58.0 8.1 %collective-permute-done.6 = f32[1,16,1024]{2,1,0:T(8,128)S(1)} collective-permute-done((f32[1,16,1024]{2,1,0:T(8,128)S(1)}, f32[1,16,1024]{2,1,0:T(8,128)S(1)}, u32[]{:S(2)}, u32[]{:S(2)}) %collective-permute-start.6) | collective-permute-done | bytes 65568 | tf_op jit(solution)/shard_map/ppermute | solution.py:27
  66.1 7.9 %collective-permute-done.7 = f32[1,16,1024]{2,1,0:T(8,128)S(1)} collective-permute-done((f32[1,16,1024]{2,1,0:T(8,128)S(1)}, f32[1,16,1024]{2,1,0:T(8,128)S(1)}, u32[]{:S(2)}, u32[]{:S(2)}) %collective-permute-start.7) | collective-permute-done | bytes 65568 | tf_op jit(solution)/shard_map/ppermute | solution.py:27
  73.9 7.9 %collective-permute-done.8 = f32[1,16,1024]{2,1,0:T(8,128)S(1)} collective-permute-done((f32[1,16,1024]{2,1,0:T(8,128)S(1)}, f32[1,16,1024]{2,1,0:T(8,128)S(1)}, u32[]{:S(2)}, u32[]{:S(2)}) %collective-permute-start.8) | collective-permute-done | bytes 65568 | tf_op jit(solution)/shard_map/ppermute | solution.py:27
  81.8 7.9 %collective-permute-done.9 = f32[1,16,1024]{2,1,0:T(8,128)S(1)} collective-permute-done((f32[1,16,1024]{2,1,0:T(8,128)S(1)}, f32[1,16,1024]{2,1,0:T(8,128)S(1)}, u32[]{:S(2)}, u32[]{:S(2)}) %collective-permute-start.9) | collective-permute-done | bytes 65568 | tf_op jit(solution)/shard_map/ppermute | solution.py:27
  89.7 7.9 %collective-permute-done.10 = f32[1,16,1024]{2,1,0:T(8,128)S(1)} collective-permute-done((f32[1,16,1024]{2,1,0:T(8,128)S(1)}, f32[1,16,1024]{2,1,0:T(8,128)S(1)}, u32[]{:S(2)}, u32[]{:S(2)}) %collective-permute-start.10) | collective-permute-done | bytes 65568 | tf_op jit(solution)/shard_map/ppermute | solution.py:27
  97.5 7.9 %collective-permute-done.11 = f32[1,16,1024]{2,1,0:T(8,128)S(1)} collective-permute-done((f32[1,16,1024]{2,1,0:T(8,128)S(1)}, f32[1,16,1024]{2,1,0:T(8,128)S(1)}, u32[]{:S(2)}, u32[]{:S(2)}) %collective-permute-start.11) | collective-permute-done | bytes 65568 | tf_op jit(solution)/shard_map/ppermute | solution.py:27
  105.4 8.2 %collective-permute-done.12 = f32[1,16,1024]{2,1,0:T(8,128)S(1)} collective-permute-done((f32[1,16,1024]{2,1,0:T(8,128)S(1)}, f32[1,16,1024]{2,1,0:T(8,128)S(1)}, u32[]{:S(2)}, u32[]{:S(2)}) %collective-permute-start.12) | collective-permute-done | bytes 65568 | tf_op jit(solution)/shard_map/ppermute | solution.py:27
  113.6 7.9 %collective-permute-done.13 = f32[1,16,1024]{2,1,0:T(8,128)S(1)} collective-permute-done((f32[1,16,1024]{2,1,0:T(8,128)S(1)}, f32[1,16,1024]{2,1,0:T(8,128)S(1)}, u32[]{:S(2)}, u32[]{:S(2)}) %collective-permute-start.13) | collective-permute-done | bytes 65568 | tf_op jit(solution)/shard_map/ppermute | solution.py:27
  121.5 7.9 %collective-permute-done.14 = f32[1,16,1024]{2,1,0:T(8,128)S(1)} collective-permute-done((f32[1,16,1024]{2,1,0:T(8,128)S(1)}, f32[1,16,1024]{2,1,0:T(8,128)S(1)}, u32[]{:S(2)}, u32[]{:S(2)}) %collective-permute-start.14) | collective-permute-done | bytes 65568 | tf_op jit(solution)/shard_map/ppermute | solution.py:27
  136.6 5.6 fusion.5
  142.1 37.6 %all-gather.2 = f32[32,1,512]{2,1,0:T(1,128)S(1)} all-gather(f32[1,1,512]{2,1,0:T(1,128)S(1)} %bitcast.67), channel_id=2, replica_groups=mesh['row'=16,'col'=2] {'row','col'}, dimensions={0}, use_global_device_ids=true | all-gather | bytes 67584 | tf_op jit(solution)/shard_map/all_gather | solution.py:36
  179.8 30.6 %convolution_bitcast_fusion.1 = f32[1024,1]{1,0:T(8,128)} fusion(f32[8192,1]{0,1:T(1,128)S(1)} %bitcast.63, f32[1024,8192]{1,0:T(8,128)} %param.17), kind=kOutput, calls=%fused_computation.16 | convolution fusion | flops 100663296 | bytes 33591296 | tf_op jit(solution)/shard_map/dot_general | solution.py:51
  210.4 47.2 %all-gather.6.cloned.1.call-done = f32[16384,256]{1,0:T(8,128)} async-done(((f32[512,256]{1,0:T(8,128)}), f32[16384,256]{1,0:T(8,128)}) %all-gather.6.cloned.1.call-update) | async-done | bytes 16777232 | tf_op jit(solution)/shard_map/all_gather | solution.py:35
  257.7 58.3 %fusion.3 = f32[1024,8192]{1,0:T(8,128)} fusion(f32[1024,256]{0,1:T(8,128)} %all-gather.8.cloned.1.call-done, f32[16384,256]{1,0:T(8,128)} %all-gather.6.cloned.1.call-done, s32[]{:T(128)S(6)} %select_n.19), kind=kOutput, calls=%fused_computation.4 | convolution fusion | flops 25769803776 | bytes 42991620 | tf_op jit(solution)/shard_map/mkv,nv->mkn/dot_general | solution.py:42
  316.0 32.9 %fusion.14 = f32[1024,1,256]{2,0,1:T(8,128)} fusion(f32[16384,256]{1,0:T(8,128)} %all-gather.6.cloned.1.call-done, s32[]{:T(128)S(6)} %select_n.19, f32[1024,8192]{1,0:T(8,128)} %fusion.3, f32[1024,8192]{1,0:T(8,128)} %param.16), kind=kOutput, calls=%fused_computation.14 | convolution fusion | flops 25778192384 | bytes 76546048 | tf_op jit(solution)/shard_map/mkn,nv->mkv/dot_general | solution.py:50
  350.0 5.6 reduce-scatter.8.cloned.1.call-done
  355.7 4.5 convolution_bitcast_fusion
  360.2 4.5 fusion.19
  364.7 3.6 copy.40
  369.7 112.4 %all-reduce.4.cloned.1.call-done = f32[256,1,1024]{2,1,0:T(1,128)} async-done(((f32[256,1,1024]{2,1,0:T(1,128)}), f32[256,1,1024]{2,1,0:T(1,128)}) %all-reduce.4.cloned.1.call-update) | async-done | bytes 1048592
  483.0 6.1 %copy.48 = f32[16,1,1024]{1,0,2:T(8,128)} copy(f32[16,1,1024]{2,1,0:T(1,128)S(1)} %constant_dynamic-slice_fusion) | data formatting | bytes 131072
  489.0 6.5 %bitcast_reduce_fusion = f32[1024,16]{1,0:T(8,128)} fusion(f32[16,1,1024]{1,0,2:T(8,128)} %copy.48), kind=kLoop, calls=%fused_computation.2 | loop fusion | bytes 131072
  496.9 5.8 reduce-scatter.12.cloned.1.call-done
  502.7 3.5 reshape_bitcast_fusion
  509.8 40.6 %all-reduce.1 = (f32[1]{0:T(128)}, f32[1]{0:T(128)}) all-reduce(f32[1]{0:T(128)} %bitcast.17, f32[1]{0:T(128)} %bitcast.18), channel_id=1, replica_groups=mesh['row'=16,'col'=2] {'row','col'}, use_global_device_ids=true, to_apply=%region_6.7 | all-reduce | flops 2 | bytes 16 | tf_op jit(solution)/shard_map/psum | solution.py:67
  552.5 40.4 %psum.23 = f32[1]{0:T(128)} all-reduce(f32[1]{0:T(128)} %bitcast.21), channel_id=1, replica_groups=mesh['row'=16,'col'=2] {'row','col'}, use_global_device_ids=true, to_apply=%region_10.11 | all-reduce | flops 1 | bytes 8 | tf_op jit(solution)/shard_map/psum | solution.py:78
  (91 shorter events, 21.0 us)
Async XLA Ops:
  7.2 203.3 %all-gather.8.cloned.1.call-start = ((), (), s32[]{:S(2)}) async-start(), calls=%async_computation.5 | async-start | bytes 1572864 | tf_op jit(solution)/shard_map/all_gather | solution.py:44
  9.4 9.2 %collective-permute-start = (f32[1,16,1024]{2,1,0:T(8,128)S(1)}, f32[1,16,1024]{2,1,0:T(8,128)S(1)}, u32[]{:S(2)}, u32[]{:S(2)}) collective-permute-start(f32[1,16,1024]{2,1,0:T(8,128)S(1)} %all_gather.12), channel_id=1, source_target_pairs={{0,2},{2,4},{4,6},{6,8},{8,10},{10,12},{12,14},{14,16},{16,18},{18... | collective-permute-start | bytes 196616 | tf_op jit(solution)/shard_map/ppermute | solution.py:27
  18.6 7.9 %collective-permute-start.1 = (f32[1,16,1024]{2,1,0:T(8,128)S(1)}, f32[1,16,1024]{2,1,0:T(8,128)S(1)}, u32[]{:S(2)}, u32[]{:S(2)}) collective-permute-start(f32[1,16,1024]{2,1,0:T(8,128)S(1)} %collective-permute-done), channel_id=1, source_target_pairs={{0,2},{2,4},{4,6},{6,8},{8,10},{10,12},{12,14},{14,16},{16,18},{18... | collective-permute-start | bytes 196616 | tf_op jit(solution)/shard_map/ppermute | solution.py:27
  26.5 7.9 %collective-permute-start.2 = (f32[1,16,1024]{2,1,0:T(8,128)S(1)}, f32[1,16,1024]{2,1,0:T(8,128)S(1)}, u32[]{:S(2)}, u32[]{:S(2)}) collective-permute-start(f32[1,16,1024]{2,1,0:T(8,128)S(1)} %collective-permute-done.1), channel_id=1, source_target_pairs={{0,2},{2,4},{4,6},{6,8},{8,10},{10,12},{12,14},{14,16},{16,18},{18... | collective-permute-start | bytes 196616 | tf_op jit(solution)/shard_map/ppermute | solution.py:27
  34.4 7.9 %collective-permute-start.3 = (f32[1,16,1024]{2,1,0:T(8,128)S(1)}, f32[1,16,1024]{2,1,0:T(8,128)S(1)}, u32[]{:S(2)}, u32[]{:S(2)}) collective-permute-start(f32[1,16,1024]{2,1,0:T(8,128)S(1)} %collective-permute-done.2), channel_id=1, source_target_pairs={{0,2},{2,4},{4,6},{6,8},{8,10},{10,12},{12,14},{14,16},{16,18},{18... | collective-permute-start | bytes 196616 | tf_op jit(solution)/shard_map/ppermute | solution.py:27
  42.2 7.9 %collective-permute-start.4 = (f32[1,16,1024]{2,1,0:T(8,128)S(1)}, f32[1,16,1024]{2,1,0:T(8,128)S(1)}, u32[]{:S(2)}, u32[]{:S(2)}) collective-permute-start(f32[1,16,1024]{2,1,0:T(8,128)S(1)} %collective-permute-done.3), channel_id=1, source_target_pairs={{0,2},{2,4},{4,6},{6,8},{8,10},{10,12},{12,14},{14,16},{16,18},{18... | collective-permute-start | bytes 196616 | tf_op jit(solution)/shard_map/ppermute | solution.py:27
  50.1 7.9 %collective-permute-start.5 = (f32[1,16,1024]{2,1,0:T(8,128)S(1)}, f32[1,16,1024]{2,1,0:T(8,128)S(1)}, u32[]{:S(2)}, u32[]{:S(2)}) collective-permute-start(f32[1,16,1024]{2,1,0:T(8,128)S(1)} %collective-permute-done.4), channel_id=1, source_target_pairs={{0,2},{2,4},{4,6},{6,8},{8,10},{10,12},{12,14},{14,16},{16,18},{18... | collective-permute-start | bytes 196616 | tf_op jit(solution)/shard_map/ppermute | solution.py:27
  58.0 8.1 %collective-permute-start.6 = (f32[1,16,1024]{2,1,0:T(8,128)S(1)}, f32[1,16,1024]{2,1,0:T(8,128)S(1)}, u32[]{:S(2)}, u32[]{:S(2)}) collective-permute-start(f32[1,16,1024]{2,1,0:T(8,128)S(1)} %collective-permute-done.5), channel_id=1, source_target_pairs={{0,2},{2,4},{4,6},{6,8},{8,10},{10,12},{12,14},{14,16},{16,18},{18... | collective-permute-start | bytes 196616 | tf_op jit(solution)/shard_map/ppermute | solution.py:27
  66.1 7.9 %collective-permute-start.7 = (f32[1,16,1024]{2,1,0:T(8,128)S(1)}, f32[1,16,1024]{2,1,0:T(8,128)S(1)}, u32[]{:S(2)}, u32[]{:S(2)}) collective-permute-start(f32[1,16,1024]{2,1,0:T(8,128)S(1)} %collective-permute-done.6), channel_id=1, source_target_pairs={{0,2},{2,4},{4,6},{6,8},{8,10},{10,12},{12,14},{14,16},{16,18},{18... | collective-permute-start | bytes 196616 | tf_op jit(solution)/shard_map/ppermute | solution.py:27
  73.9 7.9 %collective-permute-start.8 = (f32[1,16,1024]{2,1,0:T(8,128)S(1)}, f32[1,16,1024]{2,1,0:T(8,128)S(1)}, u32[]{:S(2)}, u32[]{:S(2)}) collective-permute-start(f32[1,16,1024]{2,1,0:T(8,128)S(1)} %collective-permute-done.7), channel_id=1, source_target_pairs={{0,2},{2,4},{4,6},{6,8},{8,10},{10,12},{12,14},{14,16},{16,18},{18... | collective-permute-start | bytes 196616 | tf_op jit(solution)/shard_map/ppermute | solution.py:27
  81.8 7.9 %collective-permute-start.9 = (f32[1,16,1024]{2,1,0:T(8,128)S(1)}, f32[1,16,1024]{2,1,0:T(8,128)S(1)}, u32[]{:S(2)}, u32[]{:S(2)}) collective-permute-start(f32[1,16,1024]{2,1,0:T(8,128)S(1)} %collective-permute-done.8), channel_id=1, source_target_pairs={{0,2},{2,4},{4,6},{6,8},{8,10},{10,12},{12,14},{14,16},{16,18},{18... | collective-permute-start | bytes 196616 | tf_op jit(solution)/shard_map/ppermute | solution.py:27
  89.7 7.9 %collective-permute-start.10 = (f32[1,16,1024]{2,1,0:T(8,128)S(1)}, f32[1,16,1024]{2,1,0:T(8,128)S(1)}, u32[]{:S(2)}, u32[]{:S(2)}) collective-permute-start(f32[1,16,1024]{2,1,0:T(8,128)S(1)} %collective-permute-done.9), channel_id=1, source_target_pairs={{0,2},{2,4},{4,6},{6,8},{8,10},{10,12},{12,14},{14,16},{16,18},{18... | collective-permute-start | bytes 196616 | tf_op jit(solution)/shard_map/ppermute | solution.py:27
  97.5 7.9 %collective-permute-start.11 = (f32[1,16,1024]{2,1,0:T(8,128)S(1)}, f32[1,16,1024]{2,1,0:T(8,128)S(1)}, u32[]{:S(2)}, u32[]{:S(2)}) collective-permute-start(f32[1,16,1024]{2,1,0:T(8,128)S(1)} %collective-permute-done.10), channel_id=1, source_target_pairs={{0,2},{2,4},{4,6},{6,8},{8,10},{10,12},{12,14},{14,16},{16,18},{18... | collective-permute-start | bytes 196616 | tf_op jit(solution)/shard_map/ppermute | solution.py:27
  105.4 8.2 %collective-permute-start.12 = (f32[1,16,1024]{2,1,0:T(8,128)S(1)}, f32[1,16,1024]{2,1,0:T(8,128)S(1)}, u32[]{:S(2)}, u32[]{:S(2)}) collective-permute-start(f32[1,16,1024]{2,1,0:T(8,128)S(1)} %collective-permute-done.11), channel_id=1, source_target_pairs={{0,2},{2,4},{4,6},{6,8},{8,10},{10,12},{12,14},{14,16},{16,18},{18... | collective-permute-start | bytes 196616 | tf_op jit(solution)/shard_map/ppermute | solution.py:27
  113.6 7.9 %collective-permute-start.13 = (f32[1,16,1024]{2,1,0:T(8,128)S(1)}, f32[1,16,1024]{2,1,0:T(8,128)S(1)}, u32[]{:S(2)}, u32[]{:S(2)}) collective-permute-start(f32[1,16,1024]{2,1,0:T(8,128)S(1)} %collective-permute-done.12), channel_id=1, source_target_pairs={{0,2},{2,4},{4,6},{6,8},{8,10},{10,12},{12,14},{14,16},{16,18},{18... | collective-permute-start | bytes 196616 | tf_op jit(solution)/shard_map/ppermute | solution.py:27
  121.5 7.9 %collective-permute-start.14 = (f32[1,16,1024]{2,1,0:T(8,128)S(1)}, f32[1,16,1024]{2,1,0:T(8,128)S(1)}, u32[]{:S(2)}, u32[]{:S(2)}) collective-permute-start(f32[1,16,1024]{2,1,0:T(8,128)S(1)} %collective-permute-done.13), channel_id=1, source_target_pairs={{0,2},{2,4},{4,6},{6,8},{8,10},{10,12},{12,14},{14,16},{16,18},{18... | collective-permute-start | bytes 196616 | tf_op jit(solution)/shard_map/ppermute | solution.py:27
  121.5 9.7 %copy-start = (f32[512,1024]{1,0:T(8,128)S(1)}, f32[512,1024]{1,0:T(8,128)}, u32[]{:S(2)}) copy-start(f32[512,1024]{1,0:T(8,128)} %param.15) | copy-start | bytes 6291460
  129.8 1.3 copy-start.2
  133.9 123.8 %all-gather.6.cloned.1.call-start = ((), (), s32[]{:S(2)}) async-start(), calls=%async_computation.3 | async-start | bytes 17301504 | tf_op jit(solution)/shard_map/all_gather | solution.py:35
  134.7 214.3 %reduce-scatter.10.cloned.1.call-start = ((), (), s32[]{:S(2)}) async-start(), calls=%async_computation.6 | async-start | bytes 786432
  134.7 1.9 copy-start.1
  210.4 145.3 %reduce-scatter.8.cloned.1.call-start = ((), (), s32[]{:S(2)}) async-start(), calls=%async_computation.4 | async-start | bytes 1572864 | tf_op jit(solution)/shard_map/reduce_scatter | solution.py:53
  348.9 133.2 %all-reduce.4.cloned.1.call-start = ((), (), s32[]{:S(2)}) async-start(), calls=%async_computation.8 | async-start | bytes 2097152
  364.7 3.7 copy-start.7
  368.4 134.3 %reduce-scatter.12.cloned.1.call-start = ((), (), s32[]{:S(2)}) async-start(), calls=%async_computation.7 | async-start | bytes 786432
  489.0 7.1 %copy-start.3 = (f32[1,16,512]{2,1,0:T(8,128)S(1)}, f32[1,16,512]{2,1,0:T(8,128)}, u32[]{:S(2)}) copy-start(f32[1,16,512]{2,1,0:T(8,128)} %param.9) | copy-start | bytes 98308
  506.1 2.9 copy-start.5
  506.1 2.9 copy-start.6
  506.1 45.6 %copy-start.4 = (f32[1,16,512]{2,1,0:T(8,128)S(1)}, f32[1,16,512]{2,1,0:T(8,128)}, u32[]{:S(2)}) copy-start(f32[1,16,512]{2,1,0:T(8,128)} %param.10) | copy-start | bytes 98308
Sparse Core Ops, SparseCore 0:
  134.0 4.8 all-gather.7
  141.8 115.8 all-gather.5
  259.9 6.1 reduce-scatter.9
  349.0 6.5 reduce-scatter.7
  368.5 113.5 all-reduce.3
  495.6 6.9 reduce-scatter.11
